TPU v7x, 32 devices: a whole 2x2x4 slice. The times are simulated.
32 devices in a mesh: dp: 8 (over z, y), tensor: 4 (over x, core).
Axes of the slice: x: 2, y: 2, z: 4, core: 2. Of those that a mesh axis runs over, the one named last changes fastest.
Arguments:
- tokens: bfloat16 [8192, 2048], P(('dp', 'tensor')), may hold values from -6 to 6
- lengths: int32 [8], P('dp'), may hold values from 256 to 1024, as said below
- attn_gain: bfloat16 [2048], replicated, may hold values from 0.25 to 1.75
- w_query: bfloat16 [2048, 2048], P('dp', 'tensor'), may hold values from -0.125 to 0.125
- w_key: bfloat16 [2048, 512], P('dp', 'tensor'), may hold values from -0.125 to 0.125
- w_value: bfloat16 [2048, 512], P('dp', 'tensor'), may hold values from -0.125 to 0.125
- w_output: bfloat16 [2048, 2048], P('tensor', 'dp'), may hold values from -1 to 1
- mlp_gain: bfloat16 [2048], replicated, may hold values from 0.25 to 1.75
- w_gate: bfloat16 [2048, 8192], P('dp', 'tensor'), may hold values from -0.125 to 0.125
- w_up: bfloat16 [2048, 8192], P('dp', 'tensor'), may hold values from -0.125 to 0.125
- w_down: bfloat16 [8192, 2048], P('tensor', 'dp'), may hold values from -0.125 to 0.125
- cotangent: bfloat16 [8192, 2048], P(('dp', 'tensor')), may hold values from -6 to 6
Outputs:
- layer_out: bfloat16 [8192, 2048], P(('dp', 'tensor'))
- grad_tokens: float32 [8192, 2048], P(('dp', 'tensor'))
- grad_query: float32 [2048, 2048], P('dp', 'tensor')
- grad_key: float32 [2048, 512], P('dp', 'tensor')
- grad_value: float32 [2048, 512], P('dp', 'tensor')
- grad_output: float32 [2048, 2048], P('tensor', 'dp')
- grad_gate: float32 [2048, 8192], P('dp', 'tensor')
- grad_up: float32 [2048, 8192], P('dp', 'tensor')
- grad_down: float32 [8192, 2048], P('tensor', 'dp')
- grad_attn_gain: float32 [2048], P(('dp', 'tensor'))
- grad_mlp_gain: float32 [2048], P(('dp', 'tensor'))
Inputs may be any that keep to these rules, and one draw needn't show every extreme that they name: `lengths`: each of the 8 sequences has a valid length from 256 to 1024; at least one has length exactly 1024.
All inputs are finite; a program needn't handle non-finite values.
Results may differ from a plain program's by a relative error of at most 0.015.
Values may be sent and summed in bfloat16 or wider, within the bound.
A program may use at most 192 MiB of HBM per device.

v0:
```python
import jax
import jax.numpy as jnp
from jax import lax
from jax.sharding import PartitionSpec as P

HD = 64
LEN = 1024
epsilon = 1e-05
theta = 500000.0


def rope_frequencies():
    half_size = HD // 2
    base_freq = theta ** (-(jnp.arange(half_size, dtype=jnp.float32) * 2.0) / HD)
    wavelength = 2.0 * jnp.pi / base_freq
    smooth = (8192.0 / wavelength - 1.0) / 3.0
    middle = (1.0 - smooth) * base_freq / 32.0 + smooth * base_freq
    return jnp.where(
        wavelength < 2048.0, base_freq, jnp.where(wavelength > 8192.0, base_freq / 32.0, middle)
    )


def rope_tables(positions):
    frequency = rope_frequencies()
    angles = positions.astype(jnp.float32)[:, None] * frequency[None, :]
    angles = jnp.concatenate([angles, angles], axis=1)
    return (jnp.cos(angles), jnp.sin(angles))


def rotate_half(vector):
    half_size = vector.shape[-1] // 2
    return jnp.concatenate([-vector[..., half_size:], vector[..., :half_size]], axis=-1)


def rope_apply(vector, cosine_table, sine_table):
    return vector * cosine_table[:, None, :] + rotate_half(vector) * sine_table[:, None, :]


def rope_back(grads, cosine_table, sine_table):
    return grads * cosine_table[:, None, :] - rotate_half(grads * sine_table[:, None, :])


def gather_attention(w_query, w_key, w_value, w_output):
    return (
        lax.all_gather(w_query, "dp", axis=0, tiled=True),
        lax.all_gather(w_key, "dp", axis=0, tiled=True),
        lax.all_gather(w_value, "dp", axis=0, tiled=True),
        lax.all_gather(w_output, "dp", axis=1, tiled=True),
    )


def gather_mlp(w_gate, w_up, w_down):
    return (
        lax.all_gather(w_gate, "dp", axis=0, tiled=True),
        lax.all_gather(w_up, "dp", axis=0, tiled=True),
        lax.all_gather(w_down, "dp", axis=1, tiled=True),
    )


def add_rows(accum, piece):
    return accum + piece


def block_scores(queries, key_vecs, lengths, block_index, block_rows):
    per_seq = LEN // block_rows
    sequence = block_index // per_seq
    row_start = block_index * block_rows
    query_blk = lax.dynamic_slice_in_dim(queries, row_start, block_rows, 0)
    length = lax.dynamic_index_in_dim(lengths, sequence, 0, keepdims=False)
    scores = jnp.einsum(
        "qkrd,jkd->krqj", query_blk, key_vecs, preferred_element_type=jnp.float32
    ) * HD ** (-0.5)
    query_pos = row_start % LEN + jnp.arange(block_rows)
    key_pos = jnp.arange(LEN)
    allowed = (key_pos[None, :] <= query_pos[:, None]) & (key_pos[None, :] < length)
    return (jnp.where(allowed, scores, -1e30), sequence, row_start, query_blk, key_vecs)


def attend(queries, key_vecs, values, lengths):
    total_rows = queries.shape[0]
    block_rows = min(512, LEN)
    blocks = total_rows // block_rows

    def one_block(block_index):
        scores, sequence, row_start, query_blk, key_seq = block_scores(
            queries, key_vecs, lengths, block_index, block_rows
        )
        row_max = jnp.max(scores, axis=-1, keepdims=True)
        exp_scores = jnp.exp(scores - row_max)
        denom = jnp.sum(exp_scores, axis=-1, keepdims=True)
        soft_low = (exp_scores / denom).astype(jnp.bfloat16)
        result = jnp.einsum("krqj,jkd->qkrd", soft_low, values, preferred_element_type=jnp.float32)
        return (result, row_max[..., 0] + jnp.log(denom[..., 0]))

    results, logsum = lax.map(one_block, jnp.arange(blocks, dtype=jnp.int32))
    return (results.reshape((total_rows,) + queries.shape[1:]), logsum)


def attend_back(queries, key_vecs, values, grad_heads, logsum, lengths):
    total_rows = queries.shape[0]
    block_rows = min(512, LEN)
    blocks = total_rows // block_rows

    def one_block(carry, item):
        key_acc, value_acc = carry
        block_index, logsum_blk = item
        scores, sequence, row_start, query_blk, key_seq = block_scores(
            queries, key_vecs, lengths, block_index, block_rows
        )
        grad_blk = lax.dynamic_slice_in_dim(grad_heads, row_start, block_rows, 0)
        soft_weights = jnp.exp(scores - logsum_blk[..., None])
        grad_soft = jnp.einsum(
            "qkrd,jkd->krqj", grad_blk, values, preferred_element_type=jnp.float32
        )
        inner_sum = jnp.sum(soft_weights * grad_soft, axis=-1, keepdims=True)
        grad_scores = (soft_weights * (grad_soft - inner_sum)).astype(jnp.bfloat16)
        grad_query = jnp.einsum(
            "krqj,jkd->qkrd", grad_scores, key_seq, preferred_element_type=jnp.float32
        ) * HD ** (-0.5)
        grad_keyblk = jnp.einsum(
            "krqj,qkrd->jkd", grad_scores, query_blk, preferred_element_type=jnp.float32
        ) * HD ** (-0.5)
        grad_valblk = jnp.einsum(
            "krqj,qkrd->jkd",
            soft_weights.astype(jnp.bfloat16),
            grad_blk,
            preferred_element_type=jnp.float32,
        )
        key_acc = add_rows(key_acc, grad_keyblk)
        value_acc = add_rows(value_acc, grad_valblk)
        return ((key_acc, value_acc), grad_query)

    zero_keys = jnp.zeros(key_vecs.shape, jnp.float32)
    (grad_keys, grad_values), grad_queries = lax.scan(
        one_block, (zero_keys, zero_keys), (jnp.arange(blocks, dtype=jnp.int32), logsum)
    )
    return (grad_queries.reshape((total_rows,) + queries.shape[1:]), grad_keys, grad_values)


def body(
    tokens,
    lengths,
    attn_gain,
    w_query,
    w_key,
    w_value,
    w_output,
    mlp_gain,
    w_gate,
    w_up,
    w_down,
    cotangent,
):
    local_rows = tokens.shape[0]
    token_full = tokens.astype(jnp.float32)
    gain_attn = attn_gain.astype(jnp.float32)
    gain_mlp = mlp_gain.astype(jnp.float32)
    inv_first = lax.rsqrt(jnp.mean(token_full * token_full, axis=1, keepdims=True) + epsilon)
    normed_attn = (token_full * inv_first * gain_attn).astype(jnp.bfloat16)
    rows_attn = lax.all_gather(normed_attn, "tensor", axis=0, tiled=True)
    group_rows = rows_attn.shape[0]
    cosine_table, sine_table = rope_tables(jnp.arange(group_rows) % LEN)
    query_all, key_all, value_all, output_all = gather_attention(w_query, w_key, w_value, w_output)
    heads_local = query_all.shape[1] // HD
    kv_local = key_all.shape[1] // HD
    query_pre = jnp.dot(rows_attn, query_all, preferred_element_type=jnp.float32)
    key_pre = jnp.dot(rows_attn, key_all, preferred_element_type=jnp.float32)
    values = (
        jnp.dot(rows_attn, value_all, preferred_element_type=jnp.float32)
        .astype(jnp.bfloat16)
        .reshape(group_rows, kv_local, HD)
    )
    queries = rope_apply(
        query_pre.reshape(group_rows, heads_local, HD), cosine_table, sine_table
    ).astype(jnp.bfloat16)
    queries = queries.reshape(group_rows, kv_local, heads_local // kv_local, HD)
    key_vecs = rope_apply(
        key_pre.reshape(group_rows, kv_local, HD), cosine_table, sine_table
    ).astype(jnp.bfloat16)
    head_full, logsum = attend(queries, key_vecs, values, lengths)
    head_out = head_full.reshape(group_rows, heads_local * HD).astype(jnp.bfloat16)
    picked = head_out
    attn_branch = lax.psum_scatter(
        jnp.dot(picked, output_all, preferred_element_type=jnp.float32),
        "tensor",
        scatter_dimension=0,
        tiled=True,
    )
    hidden = token_full + attn_branch
    inv_second = lax.rsqrt(jnp.mean(hidden * hidden, axis=1, keepdims=True) + epsilon)
    normed_mlp = (hidden * inv_second * gain_mlp).astype(jnp.bfloat16)
    rows_mlp = lax.all_gather(normed_mlp, "tensor", axis=0, tiled=True)
    gate_all, up_all, down_all = gather_mlp(w_gate, w_up, w_down)
    gate_proj = jnp.dot(rows_mlp, gate_all, preferred_element_type=jnp.float32)
    up_proj = jnp.dot(rows_mlp, up_all, preferred_element_type=jnp.float32)
    gate_sig = jax.nn.sigmoid(gate_proj)
    activated = (gate_proj * gate_sig * up_proj).astype(jnp.bfloat16)
    picked = activated
    mlp_branch = lax.psum_scatter(
        jnp.dot(picked, down_all, preferred_element_type=jnp.float32).astype(jnp.bfloat16),
        "tensor",
        scatter_dimension=0,
        tiled=True,
    ).astype(jnp.float32)
    layer_out = (hidden + mlp_branch).astype(jnp.bfloat16)
    group_row = lax.axis_index("tensor") * local_rows + jnp.arange(local_rows)
    row_seq = group_row // LEN
    row_pos = group_row % LEN
    seq_ids = jnp.arange(lengths.shape[0])
    row_len = jnp.sum(jnp.where(row_seq[:, None] == seq_ids[None, :], lengths[None, :], 0), axis=1)
    valid_rows = (row_pos < row_len).astype(jnp.float32)
    cot_masked = cotangent.astype(jnp.float32) * valid_rows[:, None]
    gate_all, up_all, down_all = gather_mlp(w_gate, w_up, w_down)
    grad_branch = lax.all_gather(cot_masked.astype(jnp.bfloat16), "tensor", axis=0, tiled=True)
    grad_down = jnp.einsum("gf,gd->fd", activated, grad_branch, preferred_element_type=jnp.float32)
    grad_act = jnp.einsum("gd,fd->gf", grad_branch, down_all, preferred_element_type=jnp.float32)
    grad_gate_pre = (grad_act * up_proj * gate_sig * (1.0 + gate_proj * (1.0 - gate_sig))).astype(
        jnp.bfloat16
    )
    grad_up_pre = (grad_act * gate_proj * gate_sig).astype(jnp.bfloat16)
    grad_gate = jnp.einsum("gd,gf->df", rows_mlp, grad_gate_pre, preferred_element_type=jnp.float32)
    grad_up = jnp.einsum("gd,gf->df", rows_mlp, grad_up_pre, preferred_element_type=jnp.float32)
    grad_gate, grad_up, grad_down = (
        lax.psum_scatter(grad_gate, "dp", scatter_dimension=0, tiled=True),
        lax.psum_scatter(grad_up, "dp", scatter_dimension=0, tiled=True),
        lax.psum_scatter(grad_down, "dp", scatter_dimension=1, tiled=True),
    )
    grad_norm_two = lax.psum_scatter(
        jnp.einsum("gf,df->gd", grad_gate_pre, gate_all, preferred_element_type=jnp.float32)
        + jnp.einsum("gf,df->gd", grad_up_pre, up_all, preferred_element_type=jnp.float32),
        "tensor",
        scatter_dimension=0,
        tiled=True,
    )
    scaled_two = grad_norm_two * gain_mlp
    gain_two_part = jnp.sum(grad_norm_two * hidden * inv_second, axis=0)
    grad_hidden = (
        cot_masked
        + inv_second * scaled_two
        - hidden * inv_second**3 * jnp.mean(scaled_two * hidden, axis=1, keepdims=True)
    )
    query_all, key_all, value_all, output_all = gather_attention(w_query, w_key, w_value, w_output)
    grad_attn = lax.all_gather(grad_hidden.astype(jnp.bfloat16), "tensor", axis=0, tiled=True)
    grad_output = jnp.einsum("gh,gd->hd", head_out, grad_attn, preferred_element_type=jnp.float32)
    grad_heads = jnp.einsum(
        "gd,hd->gh", grad_attn, output_all, preferred_element_type=jnp.float32
    ).astype(jnp.bfloat16)
    grad_heads = grad_heads.reshape(group_rows, kv_local, heads_local // kv_local, HD)
    grad_queries, grad_keys, grad_values = attend_back(
        queries, key_vecs, values, grad_heads, logsum, lengths
    )
    grad_qpre = rope_back(
        grad_queries.reshape(group_rows, heads_local, HD), cosine_table, sine_table
    )
    grad_qpre = grad_qpre.astype(jnp.bfloat16).reshape(group_rows, heads_local * HD)
    grad_kpre = (
        rope_back(grad_keys, cosine_table, sine_table)
        .astype(jnp.bfloat16)
        .reshape(group_rows, kv_local * HD)
    )
    grad_vpre = grad_values.astype(jnp.bfloat16).reshape(group_rows, kv_local * HD)
    grad_query = jnp.einsum("gd,gh->dh", rows_attn, grad_qpre, preferred_element_type=jnp.float32)
    grad_key = jnp.einsum("gd,gh->dh", rows_attn, grad_kpre, preferred_element_type=jnp.float32)
    grad_value = jnp.einsum("gd,gh->dh", rows_attn, grad_vpre, preferred_element_type=jnp.float32)
    grad_query, grad_key, grad_value, grad_output = (
        lax.psum_scatter(grad_query, "dp", scatter_dimension=0, tiled=True),
        lax.psum_scatter(grad_key, "dp", scatter_dimension=0, tiled=True),
        lax.psum_scatter(grad_value, "dp", scatter_dimension=0, tiled=True),
        lax.psum_scatter(grad_output, "dp", scatter_dimension=1, tiled=True),
    )
    grad_norm_one = lax.psum_scatter(
        jnp.einsum("gh,dh->gd", grad_qpre, query_all, preferred_element_type=jnp.float32)
        + jnp.einsum("gh,dh->gd", grad_kpre, key_all, preferred_element_type=jnp.float32)
        + jnp.einsum("gh,dh->gd", grad_vpre, value_all, preferred_element_type=jnp.float32),
        "tensor",
        scatter_dimension=0,
        tiled=True,
    )
    scaled_one = grad_norm_one * gain_attn
    gain_one_part = jnp.sum(grad_norm_one * token_full * inv_first, axis=0)
    grad_tokens = (
        grad_hidden
        + inv_first * scaled_one
        - token_full * inv_first**3 * jnp.mean(scaled_one * token_full, axis=1, keepdims=True)
    )
    grad_attn_gain, grad_mlp_gain = (
        lax.psum_scatter(gain_one_part, ("dp", "tensor"), scatter_dimension=0, tiled=True),
        lax.psum_scatter(gain_two_part, ("dp", "tensor"), scatter_dimension=0, tiled=True),
    )
    return (
        layer_out,
        grad_tokens,
        grad_query,
        grad_key,
        grad_value,
        grad_output,
        grad_gate,
        grad_up,
        grad_down,
        grad_attn_gain,
        grad_mlp_gain,
    )


def solution(mesh):
    in_specs = (
        P(("dp", "tensor"), None),
        P("dp"),
        P(),
        P("dp", "tensor"),
        P("dp", "tensor"),
        P("dp", "tensor"),
        P("tensor", "dp"),
        P(),
        P("dp", "tensor"),
        P("dp", "tensor"),
        P("tensor", "dp"),
        P(("dp", "tensor"), None),
    )
    out_specs = (
        P(("dp", "tensor"), None),
        P(("dp", "tensor"), None),
        P("dp", "tensor"),
        P("dp", "tensor"),
        P("dp", "tensor"),
        P("tensor", "dp"),
        P("dp", "tensor"),
        P("dp", "tensor"),
        P("tensor", "dp"),
        P(("dp", "tensor")),
        P(("dp", "tensor")),
    )
    return jax.shard_map(body, mesh=mesh, in_specs=in_specs, out_specs=out_specs, check_vma=False)
```

profile of v0, /device:TPU:0, one launch (start us, length us, event | category | flops | bytes accessed | tf_op | source)
XLA Modules:
  0.0 2289.9 jit_solution(13640120241173803262)
XLA Ops:
  15.9 33.1 %all_gather.42 = bf16[2048,128]{1,0:T(8,128)(2,1)S(1)} all-gather(bf16[256,128]{1,0:T(8,128)(2,1)S(1)} %copy-done.27), channel_id=1, replica_groups=mesh['dp'=8,'tensor'=4] {'dp'}, dimensions={0}, use_global_device_ids=true | all-gather | bytes 589824 | tf_op jit(solution)/shard_map/all_gather | solution.py:46
  49.0 31.9 %all_gather.43 = bf16[2048,128]{1,0:T(8,128)(2,1)S(1)} all-gather(bf16[256,128]{1,0:T(8,128)(2,1)S(1)} %copy-done.28), channel_id=1, replica_groups=mesh['dp'=8,'tensor'=4] {'dp'}, dimensions={0}, use_global_device_ids=true | all-gather | bytes 589824 | tf_op jit(solution)/shard_map/all_gather | solution.py:47
  113.4 33.0 %while.31 = (s32[]{:T(128)}, bf16[2,512,2,4,64]{1,4,3,2,0:T(8,128)(2,1)S(1)}, f32[2,2,4,512]{3,2,1,0:T(4,128)}, s32[2]{0:T(128)S(1)}, s32[1]{0:T(128)}, /*index=...) while((s32[]{:T(128)}, ...), condition=%wide.region_4.5_spmd, body=%wide.region_1.4_spmd.sunk | while | flops 1125119488 | bytes 54663480 | solution.py:95
  162.1 69.1 %reduce-scatter.12.cloned.1.call-done = f32[256,2048]{1,0:T(8,128)} async-done(((f32[1024,2048]{1,0:T(8,128)}), f32[256,2048]{1,0:T(8,128)}) %reduce-scatter.12.cloned.1.call-update) | async-done | bytes 2097168 | tf_op jit(solution)/shard_map/reduce_scatter | solution.py:183
  239.1 118.6 %all-gather.20.cloned.1.call-done = bf16[2048,2048]{1,0:T(8,128)(2,1)} async-done(((bf16[256,2048]{1,0:T(8,128)(2,1)}), bf16[2048,2048]{1,0:T(8,128)(2,1)}) %all-gather.20.cloned.1.call-update) | async-done | bytes 8388624 | tf_op jit(solution)/shard_map/all_gather | solution.py:55
  357.7 34.7 %all-gather.16.cloned.1.call-done = bf16[1024,2048]{1,0:T(8,128)(2,1)} async-done(((bf16[256,2048]{1,0:T(8,128)(2,1)}), bf16[1024,2048]{1,0:T(8,128)(2,1)}) %all-gather.16.cloned.1.call-update) | async-done | bytes 4194320 | tf_op jit(solution)/shard_map/all_gather | solution.py:192
  407.3 111.7 %all-gather.18.cloned.1.call-done = bf16[2048,2048]{1,0:T(8,128)(2,1)} async-done(((bf16[256,2048]{1,0:T(8,128)(2,1)}), bf16[2048,2048]{1,0:T(8,128)(2,1)}) %all-gather.18.cloned.1.call-update) | async-done | bytes 8388624 | tf_op jit(solution)/shard_map/all_gather | solution.py:54
  533.5 20.3 all-gather.24.cloned.1.call-done
  553.8 127.0 %all-gather.22.cloned.1.call-done = bf16[2048,2048]{1,0:T(8,128)(2,1)} async-done(((bf16[2048,256]{1,0:T(8,128)(2,1)}), bf16[2048,2048]{1,0:T(8,128)(2,1)}) %all-gather.22.cloned.1.call-update) | async-done | bytes 8388624 | tf_op jit(solution)/shard_map/all_gather | solution.py:56
  680.8 22.1 multiply_convert_fusion
  743.5 55.7 %reduce-scatter.16.cloned.1.call-done = f32[256,2048]{1,0:T(8,128)} async-done(((f32[1024,2048]{1,0:T(8,128)}), f32[256,2048]{1,0:T(8,128)}) %reduce-scatter.16.cloned.1.call-update) | async-done | bytes 2097168 | tf_op jit(solution)/shard_map/reduce_scatter | solution.py:228
  801.9 44.4 %reduce-scatter.14.cloned.1.call-done = bf16[256,2048]{1,0:T(8,128)(2,1)} async-done(((bf16[1024,2048]{1,0:T(8,128)(2,1)}), bf16[256,2048]{1,0:T(8,128)(2,1)}) %reduce-scatter.14.cloned.1.call-update) | async-done | bytes 1048592 | tf_op jit(solution)/shard_map/reduce_scatter | solution.py:199
  851.1 34.5 %all-gather.26.cloned.1.call-done = bf16[1024,2048]{1,0:T(8,128)(2,1)} async-done(((bf16[256,2048]{1,0:T(8,128)(2,1)}), bf16[1024,2048]{1,0:T(8,128)(2,1)}) %all-gather.26.cloned.1.call-update) | async-done | bytes 4194320 | tf_op jit(solution)/shard_map/all_gather | solution.py:243
  891.8 129.4 %while.32 = (s32[]{:T(128)}, f32[1024,2,64]{0,2,1:T(8,128)S(1)}, f32[1024,2,64]{0,2,1:T(8,128)}, f32[2,512,2,4,64]{1,0,4,3,2:T(2,128)}, s32[2]{0:T(128)S(1)}, /*...) while((s32[]{:T(128)}, f32[1024,2,64]{0,2,1:T(8,128)S(1)}, ...), condition=%wide.region_12.13_spmd.clone, body=%wide.region_10.12_spmd.clone.sunk | while | flops 2749232640 | bytes 176085424 | solution.py:134
  936.5 19.6 dynamic_update_slice.28
  1001.5 19.6 dynamic_update_slice.28
  1115.1 39.9 %all-reduce.2 = (f32[2048]{0:T(1024)S(1)}, f32[2048]{0:T(1024)S(1)}) all-reduce(f32[2048]{0:T(1024)S(1)} %get-tuple-element.297, f32[2048]{0:T(1024)S(1)} %copy-done.29), channel_id=13, replica_groups=mesh['dp'=8,'tensor'=4] {'dp','tensor'}, use_global_device_ids=true, to_apply=%region_23.24.clone | all-reduce | flops 4096 | bytes 32768
  1159.7 20.7 reduce-scatter.22.cloned.1.call-done
  1180.4 67.1 %reduce-scatter.24.cloned.1.call-done = f32[256,128]{1,0:T(8,128)} async-done(((f32[2048,128]{1,0:T(8,128)}), f32[256,128]{1,0:T(8,128)}) %reduce-scatter.24.cloned.1.call-update) | async-done | bytes 131088 | tf_op jit(solution)/shard_map/reduce_scatter | solution.py:268
  1247.5 91.8 %reduce-scatter.26.cloned.1.call-done = f32[512,256]{1,0:T(8,128)} async-done(((f32[512,2048]{1,0:T(8,128)}), f32[512,256]{1,0:T(8,128)}) %reduce-scatter.26.cloned.1.call-update) | async-done | bytes 524304 | tf_op jit(solution)/shard_map/reduce_scatter | solution.py:269
  1339.2 92.0 %reduce-scatter.20.cloned.1.call-done = f32[256,512]{1,0:T(8,128)} async-done(((f32[2048,512]{1,0:T(8,128)}), f32[256,512]{1,0:T(8,128)}) %reduce-scatter.20.cloned.1.call-update) | async-done | bytes 524304 | tf_op jit(solution)/shard_map/reduce_scatter | solution.py:266
  1431.3 284.1 %reduce-scatter.30.cloned.1.call-done = f32[256,2048]{1,0:T(8,128)} async-done(((f32[2048,2048]{1,0:T(8,128)}), f32[256,2048]{1,0:T(8,128)}) %reduce-scatter.30.cloned.1.call-update) | async-done | bytes 2097168 | tf_op jit(solution)/shard_map/reduce_scatter | solution.py:225
  1715.4 283.7 %reduce-scatter.28.cloned.1.call-done = f32[256,2048]{1,0:T(8,128)} async-done(((f32[2048,2048]{1,0:T(8,128)}), f32[256,2048]{1,0:T(8,128)}) %reduce-scatter.28.cloned.1.call-update) | async-done | bytes 2097168 | tf_op jit(solution)/shard_map/reduce_scatter | solution.py:224
  1999.1 283.5 %reduce-scatter.32.cloned.1.call-done = f32[2048,256]{1,0:T(8,128)} async-done(((f32[2048,2048]{1,0:T(8,128)}), f32[2048,256]{1,0:T(8,128)}) %reduce-scatter.32.cloned.1.call-update) | async-done | bytes 2097168 | tf_op jit(solution)/shard_map/reduce_scatter | solution.py:226
  (227 shorter events, 365.3 us)
Async XLA Ops:
  7.2 73.7 %all-gather.10.cloned.1.call-start = ((), (), s32[]{:S(2)}) async-start(), calls=%async_computation.11 | async-start | bytes 5242880 | tf_op jit(solution)/shard_map/all_gather | solution.py:160
  13.2 90.1 %all-gather.12.cloned.1.call-start = ((), (), s32[]{:S(2)}) async-start(), calls=%async_computation.12 | async-start | bytes 2359296 | tf_op jit(solution)/shard_map/all_gather | solution.py:45
  13.9 140.3 %all-gather.14.cloned.1.call-start = ((), (), s32[]{:S(2)}) async-start(), calls=%async_computation.13 | async-start | bytes 2359296 | tf_op jit(solution)/shard_map/all_gather | solution.py:48
  14.7 216.5 %reduce-scatter.12.cloned.1.call-start = ((), (), s32[]{:S(2)}) async-start(), calls=%async_computation.14 | async-start | bytes 10485760 | tf_op jit(solution)/shard_map/reduce_scatter | solution.py:183
  15.8 94.5 %copy-start.9 = (f32[1024,64]{0,1:T(8,128)}, f32[1024,64]{0,1:T(8,128)S(1)}, u32[]{:S(2)}) copy-start(f32[1024,64]{0,1:T(8,128)S(1)} %get-tuple-element.360) | copy-start | bytes 786436
  15.8 94.5 %copy-start.11 = (f32[1024,64]{0,1:T(8,128)}, f32[1024,64]{0,1:T(8,128)S(1)}, u32[]{:S(2)}) copy-start(f32[1024,64]{0,1:T(8,128)S(1)} %get-tuple-element.359) | copy-start | bytes 786436
  161.4 69.8 %copy-start.2 = (bf16[256,2048]{1,0:T(8,128)(2,1)S(1)}, bf16[256,2048]{1,0:T(8,128)(2,1)}, u32[]{:S(2)}) copy-start(bf16[256,2048]{1,0:T(8,128)(2,1)} %param.16) | copy-start | bytes 3145732
  161.5 196.2 %all-gather.20.cloned.1.call-start = ((), (), s32[]{:S(2)}) async-start(), calls=%async_computation.17 | async-start | bytes 9437184 | tf_op jit(solution)/shard_map/all_gather | solution.py:55
  162.1 230.3 %all-gather.16.cloned.1.call-start = ((), (), s32[]{:S(2)}) async-start(), calls=%async_computation.15 | async-start | bytes 5242880 | tf_op jit(solution)/shard_map/all_gather | solution.py:192
  234.4 284.6 %all-gather.18.cloned.1.call-start = ((), (), s32[]{:S(2)}) async-start(), calls=%async_computation.16 | async-start | bytes 9437184 | tf_op jit(solution)/shard_map/all_gather | solution.py:54
  235.2 318.6 %all-gather.24.cloned.1.call-start = ((), (), s32[]{:S(2)}) async-start(), calls=%async_computation.20 | async-start | bytes 5242880 | tf_op jit(solution)/shard_map/all_gather | solution.py:214
  238.3 442.5 %all-gather.22.cloned.1.call-start = ((), (), s32[]{:S(2)}) async-start(), calls=%async_computation.18 | async-start | bytes 9437184 | tf_op jit(solution)/shard_map/all_gather | solution.py:56
  239.1 560.1 %reduce-scatter.16.cloned.1.call-start = ((), (), s32[]{:S(2)}) async-start(), calls=%async_computation.21 | async-start | bytes 10485760 | tf_op jit(solution)/shard_map/reduce_scatter | solution.py:228
  729.4 116.9 %reduce-scatter.14.cloned.1.call-start = ((), (), s32[]{:S(2)}) async-start(), calls=%async_computation.19 | async-start | bytes 5242880 | tf_op jit(solution)/shard_map/reduce_scatter | solution.py:199
  743.4 102.9 %copy-start.17 = (bf16[256,2048]{1,0:T(8,128)(2,1)S(1)}, bf16[256,2048]{1,0:T(8,128)(2,1)}, u32[]{:S(2)}) copy-start(bf16[256,2048]{1,0:T(8,128)(2,1)} %param.27) | copy-start | bytes 3145732
  743.4 142.2 %all-gather.26.cloned.1.call-start = ((), (), s32[]{:S(2)}) async-start(), calls=%async_computation.22 | async-start | bytes 5242880 | tf_op jit(solution)/shard_map/all_gather | solution.py:243
  851.0 261.2 %reduce-scatter.18.cloned.1.call-start = ((), (), s32[]{:S(2)}) async-start(), calls=%async_computation.23 | async-start | bytes 10485760 | tf_op jit(solution)/shard_map/reduce_scatter | solution.py:271
  1040.6 139.8 %reduce-scatter.22.cloned.1.call-start = ((), (), s32[]{:S(2)}) async-start(), calls=%async_computation.25 | async-start | bytes 1179648 | tf_op jit(solution)/shard_map/reduce_scatter | solution.py:267
  1045.2 202.3 %reduce-scatter.24.cloned.1.call-start = ((), (), s32[]{:S(2)}) async-start(), calls=%async_computation.26 | async-start | bytes 1179648 | tf_op jit(solution)/shard_map/reduce_scatter | solution.py:268
  1050.4 288.8 %reduce-scatter.26.cloned.1.call-start = ((), (), s32[]{:S(2)}) async-start(), calls=%async_computation.27 | async-start | bytes 4718592 | tf_op jit(solution)/shard_map/reduce_scatter | solution.py:269
  1058.5 372.8 %reduce-scatter.20.cloned.1.call-start = ((), (), s32[]{:S(2)}) async-start(), calls=%async_computation.24 | async-start | bytes 4718592 | tf_op jit(solution)/shard_map/reduce_scatter | solution.py:266
  1065.1 650.3 %reduce-scatter.30.cloned.1.call-start = ((), (), s32[]{:S(2)}) async-start(), calls=%async_computation.29 | async-start | bytes 18874368 | tf_op jit(solution)/shard_map/reduce_scatter | solution.py:225
  1080.5 918.6 %reduce-scatter.28.cloned.1.call-start = ((), (), s32[]{:S(2)}) async-start(), calls=%async_computation.28 | async-start | bytes 18874368 | tf_op jit(solution)/shard_map/reduce_scatter | solution.py:224
  1096.1 1186.5 %reduce-scatter.32.cloned.1.call-start = ((), (), s32[]{:S(2)}) async-start(), calls=%async_computation.30 | async-start | bytes 18874368 | tf_op jit(solution)/shard_map/reduce_scatter | solution.py:226
  (35 other events, 336.7 us)
Sparse Core Ops, SparseCore 0:
  13.3 37.1 all-gather.9
  52.6 50.5 all-gather.11
  105.3 48.8 all-gather.13
  161.6 69.5 reduce-scatter.11
  233.2 124.4 all-gather.19
  359.7 32.6 all-gather.15
  394.5 124.4 all-gather.17
  521.1 32.6 all-gather.23
  555.8 124.9 all-gather.21
  729.6 69.5 reduce-scatter.15
  801.7 44.5 reduce-scatter.13
  851.1 34.4 all-gather.25
  1040.7 71.4 reduce-scatter.17
  1116.0 64.2 reduce-scatter.21
  1184.2 63.2 reduce-scatter.23
  1251.5 87.6 reduce-scatter.25
  1343.3 87.9 reduce-scatter.19
  1435.5 279.8 reduce-scatter.29
  1719.8 279.3 reduce-scatter.27
  2003.3 279.2 reduce-scatter.31
where the time goes:
time: 2300 us; the launch traced here: 2290 us
  waiting for transfers between devices  1770 us (77%)
  matrix products  271 us (12%)
  blocking collectives  105 us (5%)
  other arithmetic  64.5 us (3%)
  local copies, waits for them, and re-layouts  62 us (3%)
    reduce_scatter x1, waiting for transfers between devices, body(): lax.psum_scatter(grad_up, 'dp', scatter_dimension=0, tiled=True)  284 us
    reduce_scatter x1, waiting for transfers between devices, body(): lax.psum_scatter(grad_gate, 'dp', scatter_dimension=0, tiled=True)  284 us
    reduce_scatter x1, waiting for transfers between devices, body(): lax.psum_scatter(grad_down, 'dp', scatter_dimension=1, tiled=True)  284 us
    all_gather x1, waiting for transfers between devices, gather_mlp(): lax.all_gather(w_down, 'dp', axis=1, tiled=True)  127 us
    all_gather x1, waiting for transfers between devices, gather_mlp(): lax.all_gather(w_up, 'dp', axis=0, tiled=True)  119 us
    all_gather x1, waiting for transfers between devices, gather_mlp(): lax.all_gather(w_gate, 'dp', axis=0, tiled=True)  112 us
    reduce_scatter x1, waiting for transfers between devices, body(): lax.psum_scatter(grad_query, 'dp', scatter_dimension=0, tiled=True)  92 us
    reduce_scatter x1, waiting for transfers between devices, body(): lax.psum_scatter(grad_output, 'dp', scatter_dimension=1, tiled=True)  91.8 us
  transfers between devices with their start and end apart: 20, of which 19 were waited for; matrix products, arithmetic and copies ran while one was open for 8% of the time, Pallas kernels for 0%

commit v1 on v0

--- a/solution.py
+++ b/solution.py
@@ -7,6 +7,19 @@
 LEN = 1024
 epsilon = 1e-05
 theta = 500000.0
+
+
+def ring_gather(array, axis, dim):
+    size, index, rows = (lax.axis_size(axis), lax.axis_index(axis), array.shape[dim])
+    ahead = [(i, (i + 1) % size) for i in range(size)]
+    out = jnp.zeros((*array.shape[:dim], size * rows, *array.shape[dim + 1 :]), array.dtype)
+    held = array
+    for step in range(size):
+        owner = (index - step) % size
+        out = lax.dynamic_update_slice_in_dim(out, held, owner * rows, axis=dim)
+        if step < size - 1:
+            held = lax.ppermute(held, axis, ahead)
+    return out
 
 
 def rope_frequencies():
@@ -52,7 +65,7 @@
 def gather_mlp(w_gate, w_up, w_down):
     return (
         lax.all_gather(w_gate, "dp", axis=0, tiled=True),
-        lax.all_gather(w_up, "dp", axis=0, tiled=True),
+        ring_gather(w_up, "dp", 0),
         lax.all_gather(w_down, "dp", axis=1, tiled=True),
     )
 

time: 2300 us -> 2230 us (0.970)
  waiting for transfers between devices: 1770 us -> 1690 us
    ppermute x0 -> x7, waiting for transfers between devices: none -> 209 us  [ring_gather(): held = lax.ppermute(held, axis, ahead)]
    all_gather x1 -> x0, waiting for transfers between devices: 119 us -> none  [gather_mlp(): lax.all_gather(w_up, 'dp', axis=0, tiled=True)]
    all_gather x1, waiting for transfers between devices: 127 us -> 42.1 us  [gather_mlp(): lax.all_gather(w_down, 'dp', axis=1, tiled=True)]
    reduce_scatter x1, waiting for transfers between devices: 69.1 us -> 0.01 us  [body(): lax.psum_scatter(jnp.dot(picked, output_all, preferred_element_type=jnp.f...]
  transfers between devices with their start and end apart: 20 -> 26, of which waited for: 19 -> 23; matrix products, arithmetic and copies ran while one was open for 8% -> 8% of each run, Pallas kernels for 0% -> 0%
where the time goes in v1:
time: 2230 us; the launch traced here: 2220 us
  waiting for transfers between devices  1690 us (76%)
  matrix products  264 us (12%)
  blocking collectives  105 us (5%)
  local copies, waits for them, and re-layouts  80.6 us (4%)
  other arithmetic  61.8 us (3%)
    reduce_scatter x1, waiting for transfers between devices, body(): lax.psum_scatter(grad_up, 'dp', scatter_dimension=0, tiled=True)  284 us
    reduce_scatter x1, waiting for transfers between devices, body(): lax.psum_scatter(grad_down, 'dp', scatter_dimension=1, tiled=True)  284 us
    reduce_scatter x1, waiting for transfers between devices, body(): lax.psum_scatter(grad_gate, 'dp', scatter_dimension=0, tiled=True)  284 us
    ppermute x7, waiting for transfers between devices, ring_gather(): held = lax.ppermute(held, axis, ahead)  209 us
    all_gather x1, waiting for transfers between devices, gather_mlp(): lax.all_gather(w_gate, 'dp', axis=0, tiled=True)  112 us
    reduce_scatter x1, waiting for transfers between devices, body(): lax.psum_scatter(grad_query, 'dp', scatter_dimension=0, tiled=True)  92 us
    reduce_scatter x1, waiting for transfers between devices, body(): lax.psum_scatter(grad_output, 'dp', scatter_dimension=1, tiled=True)  91.7 us
    reduce_scatter x1, waiting for transfers between devices, body(): lax.psum_scatter(grad_value, 'dp', scatter_dimension=0, tiled=True)  67.1 us
  transfers between devices with their start and end apart: 26, of which 23 were waited for; matrix products, arithmetic and copies ran while one was open for 8% of the time, Pallas kernels for 0%

profile of v1, /device:TPU:0, one launch (start us, length us, event | category | flops | bytes accessed | tf_op | source)
XLA Modules:
  0.0 2222.2 jit_solution(7456830558008618177)
XLA Ops:
  15.9 33.1 %all_gather.38 = bf16[2048,128]{1,0:T(8,128)(2,1)S(1)} all-gather(bf16[256,128]{1,0:T(8,128)(2,1)S(1)} %copy-done.39), channel_id=1, replica_groups=mesh['dp'=8,'tensor'=4] {'dp'}, dimensions={0}, use_global_device_ids=true | all-gather | bytes 589824 | tf_op jit(solution)/shard_map/all_gather | solution.py:59
  48.9 31.7 %all_gather.39 = bf16[2048,128]{1,0:T(8,128)(2,1)S(1)} all-gather(bf16[256,128]{1,0:T(8,128)(2,1)S(1)} %copy-done.40), channel_id=1, replica_groups=mesh['dp'=8,'tensor'=4] {'dp'}, dimensions={0}, use_global_device_ids=true | all-gather | bytes 589824 | tf_op jit(solution)/shard_map/all_gather | solution.py:60
  112.8 30.8 %while.31 = (s32[]{:T(128)}, bf16[2,512,2,4,64]{1,4,3,2,0:T(8,128)(2,1)S(1)}, f32[2,2,4,512]{3,2,1,0:T(4,128)}, s32[2]{0:T(128)S(1)}, s32[1]{0:T(128)}, /*index=...) while((s32[]{:T(128)}, ...), condition=%wide.region_4.5_spmd, body=%wide.region_1.4_spmd.sunk | while | flops 1125119488 | bytes 54663480 | solution.py:108
  167.2 25.3 %collective-permute-done = bf16[256,2048]{1,0:T(8,128)(2,1)S(1)} collective-permute-done((bf16[256,2048]{1,0:T(8,128)(2,1)S(1)}, bf16[256,2048]{1,0:T(8,128)(2,1)S(1)}, u32[]{:S(2)}, u32[]{:S(2)}) %collective-permute-start) | collective-permute-done | bytes 1048608 | tf_op jit(solution)/shard_map/ppermute | solution.py:21
  192.5 25.9 %collective-permute-done.1 = bf16[256,2048]{1,0:T(8,128)(2,1)S(1)} collective-permute-done((bf16[256,2048]{1,0:T(8,128)(2,1)S(1)}, bf16[256,2048]{1,0:T(8,128)(2,1)S(1)}, u32[]{:S(2)}, u32[]{:S(2)}) %collective-permute-start.1) | collective-permute-done | bytes 1048608 | tf_op jit(solution)/shard_map/ppermute | solution.py:21
  219.3 25.1 %collective-permute-done.2 = bf16[256,2048]{1,0:T(8,128)(2,1)} collective-permute-done((bf16[256,2048]{1,0:T(8,128)(2,1)S(1)}, bf16[256,2048]{1,0:T(8,128)(2,1)}, u32[]{:S(2)}, u32[]{:S(2)}) %collective-permute-start.2) | collective-permute-done | bytes 1048608 | tf_op jit(solution)/shard_map/ppermute | solution.py:21
  247.7 21.2 collective-permute-done.3
  268.9 40.7 %collective-permute-done.4 = bf16[256,2048]{1,0:T(8,128)(2,1)S(1)} collective-permute-done((bf16[256,2048]{1,0:T(8,128)(2,1)}, bf16[256,2048]{1,0:T(8,128)(2,1)S(1)}, u32[]{:S(2)}, u32[]{:S(2)}) %collective-permute-start.4) | collective-permute-done | bytes 1048608 | tf_op jit(solution)/shard_map/ppermute | solution.py:21
  316.1 36.4 %collective-permute-done.5 = bf16[256,2048]{1,0:T(8,128)(2,1)} collective-permute-done((bf16[256,2048]{1,0:T(8,128)(2,1)S(1)}, bf16[256,2048]{1,0:T(8,128)(2,1)}, u32[]{:S(2)}, u32[]{:S(2)}) %collective-permute-start.5) | collective-permute-done | bytes 1048608 | tf_op jit(solution)/shard_map/ppermute | solution.py:21
  362.1 34.4 %collective-permute-done.6 = bf16[256,2048]{1,0:T(8,128)(2,1)S(1)} collective-permute-done((bf16[256,2048]{1,0:T(8,128)(2,1)}, bf16[256,2048]{1,0:T(8,128)(2,1)S(1)}, u32[]{:S(2)}, u32[]{:S(2)}) %collective-permute-start.6) | collective-permute-done | bytes 1048608 | tf_op jit(solution)/shard_map/ppermute | solution.py:21
  397.6 42.1 %all-gather.19.cloned.1.call-done = bf16[2048,2048]{1,0:T(8,128)(2,1)} async-done(((bf16[2048,256]{1,0:T(8,128)(2,1)}), bf16[2048,2048]{1,0:T(8,128)(2,1)}) %all-gather.19.cloned.1.call-update) | async-done | bytes 8388624 | tf_op jit(solution)/shard_map/all_gather | solution.py:69
  454.2 112.1 %all-gather.17.cloned.1.call-done = bf16[2048,2048]{1,0:T(8,128)(2,1)} async-done(((bf16[256,2048]{1,0:T(8,128)(2,1)}), bf16[2048,2048]{1,0:T(8,128)(2,1)}) %all-gather.17.cloned.1.call-update) | async-done | bytes 8388624 | tf_op jit(solution)/shard_map/all_gather | solution.py:67
  566.3 34.8 %all-gather.15.cloned.1.call-done = bf16[1024,2048]{1,0:T(8,128)(2,1)} async-done(((bf16[256,2048]{1,0:T(8,128)(2,1)}), bf16[1024,2048]{1,0:T(8,128)(2,1)}) %all-gather.15.cloned.1.call-update) | async-done | bytes 4194320 | tf_op jit(solution)/shard_map/all_gather | solution.py:205
  676.0 57.6 %reduce-scatter.16.cloned.1.call-done = f32[256,2048]{1,0:T(8,128)} async-done(((f32[1024,2048]{1,0:T(8,128)}), f32[256,2048]{1,0:T(8,128)}) %reduce-scatter.16.cloned.1.call-update) | async-done | bytes 2097168 | tf_op jit(solution)/shard_map/reduce_scatter | solution.py:241
  736.3 44.2 %reduce-scatter.14.cloned.1.call-done = bf16[256,2048]{1,0:T(8,128)(2,1)} async-done(((bf16[1024,2048]{1,0:T(8,128)(2,1)}), bf16[256,2048]{1,0:T(8,128)(2,1)}) %reduce-scatter.14.cloned.1.call-update) | async-done | bytes 1048592 | tf_op jit(solution)/shard_map/reduce_scatter | solution.py:212
  785.4 34.5 %all-gather.23.cloned.1.call-done = bf16[1024,2048]{1,0:T(8,128)(2,1)} async-done(((bf16[256,2048]{1,0:T(8,128)(2,1)}), bf16[1024,2048]{1,0:T(8,128)(2,1)}) %all-gather.23.cloned.1.call-update) | async-done | bytes 4194320 | tf_op jit(solution)/shard_map/all_gather | solution.py:256
  826.1 127.6 %while.32 = (s32[]{:T(128)}, f32[1024,2,64]{0,2,1:T(8,128)S(1)}, f32[1024,2,64]{0,2,1:T(8,128)}, f32[2,512,2,4,64]{1,0,4,3,2:T(2,128)}, s32[2]{0:T(128)S(1)}, /*...) while((s32[]{:T(128)}, f32[1024,2,64]{0,2,1:T(8,128)S(1)}, ...), condition=%wide.region_12.13_spmd.clone, body=%wide.region_10.12_spmd.clone.sunk | while | flops 2749232640 | bytes 181328368 | solution.py:147
  1047.3 40.1 %all-reduce.2 = (f32[2048]{0:T(1024)S(1)}, f32[2048]{0:T(1024)S(1)}) all-reduce(f32[2048]{0:T(1024)S(1)} %get-tuple-element.297, f32[2048]{0:T(1024)S(1)} %copy-done.41), channel_id=13, replica_groups=mesh['dp'=8,'tensor'=4] {'dp','tensor'}, use_global_device_ids=true, to_apply=%region_23.24.clone | all-reduce | flops 4096 | bytes 32768
  1113.0 67.1 %reduce-scatter.24.cloned.1.call-done = f32[256,128]{1,0:T(8,128)} async-done(((f32[2048,128]{1,0:T(8,128)}), f32[256,128]{1,0:T(8,128)}) %reduce-scatter.24.cloned.1.call-update) | async-done | bytes 131088 | tf_op jit(solution)/shard_map/reduce_scatter | solution.py:281
  1180.0 91.7 %reduce-scatter.26.cloned.1.call-done = f32[512,256]{1,0:T(8,128)} async-done(((f32[512,2048]{1,0:T(8,128)}), f32[512,256]{1,0:T(8,128)}) %reduce-scatter.26.cloned.1.call-update) | async-done | bytes 524304 | tf_op jit(solution)/shard_map/reduce_scatter | solution.py:282
  1271.8 92.0 %reduce-scatter.20.cloned.1.call-done = f32[256,512]{1,0:T(8,128)} async-done(((f32[2048,512]{1,0:T(8,128)}), f32[256,512]{1,0:T(8,128)}) %reduce-scatter.20.cloned.1.call-update) | async-done | bytes 524304 | tf_op jit(solution)/shard_map/reduce_scatter | solution.py:279
  1363.8 284.1 %reduce-scatter.30.cloned.1.call-done = f32[256,2048]{1,0:T(8,128)} async-done(((f32[2048,2048]{1,0:T(8,128)}), f32[256,2048]{1,0:T(8,128)}) %reduce-scatter.30.cloned.1.call-update) | async-done | bytes 2097168 | tf_op jit(solution)/shard_map/reduce_scatter | solution.py:238
  1647.9 283.5 %reduce-scatter.28.cloned.1.call-done = f32[256,2048]{1,0:T(8,128)} async-done(((f32[2048,2048]{1,0:T(8,128)}), f32[256,2048]{1,0:T(8,128)}) %reduce-scatter.28.cloned.1.call-update) | async-done | bytes 2097168 | tf_op jit(solution)/shard_map/reduce_scatter | solution.py:237
  1931.4 283.8 %reduce-scatter.32.cloned.1.call-done = f32[2048,256]{1,0:T(8,128)} async-done(((f32[2048,2048]{1,0:T(8,128)}), f32[2048,256]{1,0:T(8,128)}) %reduce-scatter.32.cloned.1.call-update) | async-done | bytes 2097168 | tf_op jit(solution)/shard_map/reduce_scatter | solution.py:239
  (277 shorter events, 461.3 us)
Async XLA Ops:
  7.2 73.4 %all-gather.9.cloned.1.call-start = ((), (), s32[]{:S(2)}) async-start(), calls=%async_computation.11 | async-start | bytes 5242880 | tf_op jit(solution)/shard_map/all_gather | solution.py:173
  13.2 90.3 %all-gather.11.cloned.1.call-start = ((), (), s32[]{:S(2)}) async-start(), calls=%async_computation.12 | async-start | bytes 2359296 | tf_op jit(solution)/shard_map/all_gather | solution.py:58
  13.9 140.6 %all-gather.13.cloned.1.call-start = ((), (), s32[]{:S(2)}) async-start(), calls=%async_computation.13 | async-start | bytes 2359296 | tf_op jit(solution)/shard_map/all_gather | solution.py:61
  14.7 229.8 %reduce-scatter.12.cloned.1.call-start = ((), (), s32[]{:S(2)}) async-start(), calls=%async_computation.14 | async-start | bytes 10485760 | tf_op jit(solution)/shard_map/reduce_scatter | solution.py:196
  161.9 235.7 %all-gather.21.cloned.1.call-start = ((), (), s32[]{:S(2)}) async-start(), calls=%async_computation.19 | async-start | bytes 5242880 | tf_op jit(solution)/shard_map/all_gather | solution.py:227
  164.3 275.4 %all-gather.19.cloned.1.call-start = ((), (), s32[]{:S(2)}) async-start(), calls=%async_computation.17 | async-start | bytes 9437184 | tf_op jit(solution)/shard_map/all_gather | solution.py:69
  164.8 401.4 %all-gather.17.cloned.1.call-start = ((), (), s32[]{:S(2)}) async-start(), calls=%async_computation.16 | async-start | bytes 9437184 | tf_op jit(solution)/shard_map/all_gather | solution.py:67
  165.6 435.5 %all-gather.15.cloned.1.call-start = ((), (), s32[]{:S(2)}) async-start(), calls=%async_computation.15 | async-start | bytes 5242880 | tf_op jit(solution)/shard_map/all_gather | solution.py:205
  165.6 26.8 %collective-permute-start = (bf16[256,2048]{1,0:T(8,128)(2,1)S(1)}, bf16[256,2048]{1,0:T(8,128)(2,1)S(1)}, u32[]{:S(2)}, u32[]{:S(2)}) collective-permute-start(bf16[256,2048]{1,0:T(8,128)(2,1)S(1)} %copy-done.25), channel_id=1, source_target_pairs={{0,4},{4,8},{8,12},{12,16},{16,20},{20,24},{24,28},{28,0},{1,5},{5... | collective-permute-start | bytes 3145736 | tf_op jit(solution)/shard_map/ppermute | solution.py:21
  192.4 25.9 %collective-permute-start.1 = (bf16[256,2048]{1,0:T(8,128)(2,1)S(1)}, bf16[256,2048]{1,0:T(8,128)(2,1)S(1)}, u32[]{:S(2)}, u32[]{:S(2)}) collective-permute-start(bf16[256,2048]{1,0:T(8,128)(2,1)S(1)} %collective-permute-done), channel_id=1, source_target_pairs={{0,4},{4,8},{8,12},{12,16},{16,20},{20,24},{24,28},{28,0},{1,5},{5... | collective-permute-start | bytes 3145736 | tf_op jit(solution)/shard_map/ppermute | solution.py:21
  247.7 486.0 %reduce-scatter.16.cloned.1.call-start = ((), (), s32[]{:S(2)}) async-start(), calls=%async_computation.20 | async-start | bytes 10485760 | tf_op jit(solution)/shard_map/reduce_scatter | solution.py:241
  268.9 40.7 %collective-permute-start.4 = (bf16[256,2048]{1,0:T(8,128)(2,1)}, bf16[256,2048]{1,0:T(8,128)(2,1)S(1)}, u32[]{:S(2)}, u32[]{:S(2)}) collective-permute-start(bf16[256,2048]{1,0:T(8,128)(2,1)} %collective-permute-done.3), channel_id=1, source_target_pairs={{0,4},{4,8},{8,12},{12,16},{16,20},{20,24},{24,28},{28,0},{1,5},{5... | collective-permute-start | bytes 3145736 | tf_op jit(solution)/shard_map/ppermute | solution.py:21
  309.6 42.9 %collective-permute-start.5 = (bf16[256,2048]{1,0:T(8,128)(2,1)S(1)}, bf16[256,2048]{1,0:T(8,128)(2,1)}, u32[]{:S(2)}, u32[]{:S(2)}) collective-permute-start(bf16[256,2048]{1,0:T(8,128)(2,1)S(1)} %collective-permute-done.4), channel_id=1, source_target_pairs={{0,4},{4,8},{8,12},{12,16},{16,20},{20,24},{24,28},{28,0},{1,5},{5... | collective-permute-start | bytes 3145736 | tf_op jit(solution)/shard_map/ppermute | solution.py:21
  352.5 44.0 %collective-permute-start.6 = (bf16[256,2048]{1,0:T(8,128)(2,1)}, bf16[256,2048]{1,0:T(8,128)(2,1)S(1)}, u32[]{:S(2)}, u32[]{:S(2)}) collective-permute-start(bf16[256,2048]{1,0:T(8,128)(2,1)} %collective-permute-done.5), channel_id=1, source_target_pairs={{0,4},{4,8},{8,12},{12,16},{16,20},{20,24},{24,28},{28,0},{1,5},{5... | collective-permute-start | bytes 3145736 | tf_op jit(solution)/shard_map/ppermute | solution.py:21
  662.1 118.5 %reduce-scatter.14.cloned.1.call-start = ((), (), s32[]{:S(2)}) async-start(), calls=%async_computation.18 | async-start | bytes 5242880 | tf_op jit(solution)/shard_map/reduce_scatter | solution.py:212
  676.0 143.9 %all-gather.23.cloned.1.call-start = ((), (), s32[]{:S(2)}) async-start(), calls=%async_computation.21 | async-start | bytes 5242880 | tf_op jit(solution)/shard_map/all_gather | solution.py:256
  785.3 259.3 %reduce-scatter.18.cloned.1.call-start = ((), (), s32[]{:S(2)}) async-start(), calls=%async_computation.22 | async-start | bytes 10485760 | tf_op jit(solution)/shard_map/reduce_scatter | solution.py:284
  973.1 139.9 %reduce-scatter.22.cloned.1.call-start = ((), (), s32[]{:S(2)}) async-start(), calls=%async_computation.24 | async-start | bytes 1179648 | tf_op jit(solution)/shard_map/reduce_scatter | solution.py:280
  977.6 202.4 %reduce-scatter.24.cloned.1.call-start = ((), (), s32[]{:S(2)}) async-start(), calls=%async_computation.25 | async-start | bytes 1179648 | tf_op jit(solution)/shard_map/reduce_scatter | solution.py:281
  982.8 288.9 %reduce-scatter.26.cloned.1.call-start = ((), (), s32[]{:S(2)}) async-start(), calls=%async_computation.26 | async-start | bytes 4718592 | tf_op jit(solution)/shard_map/reduce_scatter | solution.py:282
  991.0 372.8 %reduce-scatter.20.cloned.1.call-start = ((), (), s32[]{:S(2)}) async-start(), calls=%async_computation.23 | async-start | bytes 4718592 | tf_op jit(solution)/shard_map/reduce_scatter | solution.py:279
  997.6 650.3 %reduce-scatter.30.cloned.1.call-start = ((), (), s32[]{:S(2)}) async-start(), calls=%async_computation.28 | async-start | bytes 18874368 | tf_op jit(solution)/shard_map/reduce_scatter | solution.py:238
  1012.9 918.5 %reduce-scatter.28.cloned.1.call-start = ((), (), s32[]{:S(2)}) async-start(), calls=%async_computation.27 | async-start | bytes 18874368 | tf_op jit(solution)/shard_map/reduce_scatter | solution.py:237
  1028.5 1186.7 %reduce-scatter.32.cloned.1.call-start = ((), (), s32[]{:S(2)}) async-start(), calls=%async_computation.29 | async-start | bytes 18874368 | tf_op jit(solution)/shard_map/reduce_scatter | solution.py:239
  (56 other events, 1048.1 us)
Sparse Core Ops, SparseCore 0:
  13.3 37.1 all-gather.8
  52.6 50.8 all-gather.10
  105.6 48.8 all-gather.12
  161.9 69.5 reduce-scatter.11
  233.5 34.4 all-gather.20
  269.9 169.6 all-gather.18
  441.7 124.4 all-gather.16
  568.4 32.6 all-gather.14
  662.2 71.3 reduce-scatter.15
  736.0 44.5 reduce-scatter.13
  785.4 34.4 all-gather.22
  973.2 71.3 reduce-scatter.17
  1048.6 64.2 reduce-scatter.21
  1116.8 63.2 reduce-scatter.23
  1184.1 87.6 reduce-scatter.25
  1275.8 87.9 reduce-scatter.19
  1368.0 279.8 reduce-scatter.29
  1652.1 279.2 reduce-scatter.27
  1935.8 279.3 reduce-scatter.31
